TPU v7x, 512 devices: a whole 4x8x8 slice. The times are simulated.
512 devices in a mesh: task: 4 (over y_lo), tok: 128 (over z, y_hi, x, core).
Axes of the slice: x: 4, y: 8 (y_hi: 2, y_lo: 4; y = y_hi * 4 + y_lo), z: 8, core: 2. Of those that a mesh axis runs over, the one named last changes fastest.
Arguments:
- hidden: bfloat16 [4, 4096, 3584], P('task', 'tok'), may hold values from -6 to 6
- attn_out: bfloat16 [4, 4096, 3584], P('task', 'tok'), may hold values from -6 to 6
- gain_attn: bfloat16 [3584], replicated, may hold values from 0.5 to 1.5
- gain_mlp: bfloat16 [3584], replicated, may hold values from 0.5 to 1.5
- lengths: int32 [4, 2], P('task'), may hold values from 512 to 2048
Outputs:
- gram_attn: float32 [128, 112, 896], P('tok', 'task')
- gram_mlp: float32 [128, 112, 896], P('tok', 'task')
All inputs are finite; a program needn't handle non-finite values.
Results may differ from a plain program's by a relative error of at most 0.0044.
Values may be sent and summed in bfloat16 or wider, within the bound.
No kernel may reach another device: no remote copies, remote signals or barrier semaphores. Data moves between devices by JAX's collectives and lax.ppermute only.
A program may use at most 64 MiB of HBM per device.

v0:
```python
import jax
import jax.numpy as jnp
from jax import lax
from jax.sharding import Mesh
from jax.sharding import PartitionSpec as P

TOK = ("z", "yh", "x", "core")
YRING = ("yh", "task")


def normed(values, gain):
    scale = lax.rsqrt(jnp.mean(values * values, axis=-1, keepdims=True) + 1e-06)
    return values * scale * gain.astype(jnp.float32)


def per_device(hidden, attn_out, gain_attn, gain_mlp, lengths):
    rows = hidden.shape[1]
    width = hidden.shape[2]
    n_z, n_yh, n_x, n_core = (lax.axis_size(a) for a in TOK)
    n_task = lax.axis_size("task")
    tokens = rows * n_z * n_yh * n_x * n_core
    seq_len = tokens // lengths.shape[1]
    band = width // 4
    part = band // (n_x * n_core * n_task)
    z = lax.axis_index("z")
    core = lax.axis_index("core")
    place = lax.axis_index(TOK) * rows + jnp.arange(rows, dtype=jnp.int32)
    which = lax.axis_index(TOK) * rows // seq_len
    limit = lax.dynamic_index_in_dim(lengths[0], which, keepdims=False)
    live = (place - which * seq_len < limit).astype(jnp.float32)[:, None]
    first = hidden[0].astype(jnp.float32)
    x_attn = (normed(first, gain_attn) * live).astype(jnp.bfloat16)
    mixed = first + attn_out[0].astype(jnp.float32)
    x_mlp = (normed(mixed, gain_mlp) * live).astype(jnp.bfloat16)
    both = jnp.concatenate([x_attn, x_mlp], axis=1)
    seen = lax.all_gather(both, ("z", "core"), axis=0, tiled=True)

    def tile(at):
        left = lax.dynamic_slice_in_dim(seen, at * width + z // 2 * band, band, 1)
        right = lax.dynamic_slice_in_dim(seen, at * width + z % 2 * 2 * band, 2 * band, 1)
        full = lax.dot_general(
            left, right, (((0,), (0,)), ((), ())), preferred_element_type=jnp.float32
        )
        full = full.reshape(n_x, n_core, n_task, part, n_yh, band)
        return jnp.where(core == 0, full[:, 0], full[:, 1])

    parts = jnp.stack([tile(0), tile(1)])
    parts = parts.transpose(4, 2, 1, 0, 3, 5).astype(jnp.bfloat16)
    parts = parts.reshape(n_yh * n_task * n_x * 2 * part, band)
    ring = lax.psum_scatter(parts, YRING, scatter_dimension=0, tiled=True)
    ring = ring.reshape(n_x, 2 * part, band)
    ring = lax.all_to_all(ring, "x", split_axis=0, concat_axis=0, tiled=True)
    total = ring.astype(jnp.float32).sum(axis=0) * (1.0 / tokens)
    return (total[None, :part], total[None, part:])


def solution(mesh):
    n_task = mesh.shape["task"]
    grid = Mesh(mesh.devices.reshape(n_task, 8, 2, 4, 2), ("task",) + TOK)
    return jax.shard_map(
        per_device,
        mesh=grid,
        in_specs=(P("task", TOK, None), P("task", TOK, None), P(), P(), P("task", None)),
        out_specs=(P(TOK, "task", None), P(TOK, "task", None)),
        check_vma=False,
    )
```

profile of v0, /device:TPU:24, one launch (start us, length us, event | category | flops | bytes accessed | tf_op | source)
XLA Modules:
  0.0 179.4 jit_solution(12961962622690158551)
XLA Ops:
  7.2 0.0 copy-start
  7.2 0.0 all-gather.2.cloned.1.call-start
  7.3 0.7 convert_element_type.40
  8.0 0.7 convert_element_type.45
  8.7 0.0 copy-done
  8.7 0.6 constant_dynamic-slice_fusion
  9.2 0.6 compare_convert_fusion
  9.9 1.3 fusion.10
  11.2 1.3 fusion.13
  12.4 0.8 pad_maximum_fusion
  13.2 0.0 all-gather.2.cloned.1.call-update
  13.2 0.0 reduce-scatter.2.cloned.1.call-start
  13.3 58.8 %all-gather.2.cloned.1.call-done = bf16[512,7168]{1,0:T(8,128)(2,1)} async-done(((bf16[32,7168]{1,0:T(8,128)(2,1)}), bf16[512,7168]{1,0:T(8,128)(2,1)}) %all-gather.2.cloned.1.call-update) | async-done | bytes 7340048 | tf_op jit(solution)/shard_map/all_gather | solution.py:36
  72.1 5.4 %fusion.4 = bf16[896,1792]{1,0:T(8,128)(2,1)} fusion(bf16[512,7168]{1,0:T(8,128)(2,1)} %all-gather.2.cloned.1.call-done, s32[]{:T(128)S(6)} %select_n.75, s32[]{:T(128)S(6)} %select_n.74), kind=kOutput, calls=%fused_computation.7 | convolution fusion | flops 1644167168 | bytes 5963784 | tf_op jit(solution)/shard_map/dot_general | solution.py:41
  77.5 5.9 %reshape.88 = bf16[4,2,4,28,2,896]{5,4,3,2,1,0:T(2,128)(2,1)S(1)} reshape(bf16[896,1792]{1,0:T(8,128)(2,1)} %fusion.4) | data formatting | bytes 6422528 | tf_op jit(solution)/shard_map/reshape | solution.py:44
  83.5 5.4 %fusion.6 = bf16[896,1792]{1,0:T(8,128)(2,1)} fusion(bf16[512,7168]{1,0:T(8,128)(2,1)} %all-gather.2.cloned.1.call-done, s32[]{:T(128)S(6)} %select_n.71, s32[]{:T(128)S(6)} %select_n.69), kind=kOutput, calls=%fused_computation.9 | convolution fusion | flops 1644167168 | bytes 5963784 | tf_op jit(solution)/shard_map/dot_general | solution.py:41
  88.9 7.1 %reshape.87 = bf16[4,2,4,28,2,896]{5,4,3,2,1,0:T(2,128)(2,1)} reshape(bf16[896,1792]{1,0:T(8,128)(2,1)} %fusion.6) | data formatting | bytes 6422528 | tf_op jit(solution)/shard_map/reshape | solution.py:44
  96.0 4.1 %fusion.16 = (bf16[4,1,4,28,2,896]{5,4,3,2,1,0:T(2,128)(2,1)S(1)}, bf16[4,1,4,28,2,896]{5,4,3,2,1,0:T(2,128)(2,1)S(1)}) fusion(bf16[4,2,4,28,2,896]{5,4,3,2,1,0:T(2,128)(2,1)} %reshape.87), kind=kLoop, calls=%fused_computation.31 | loop fusion | bytes 6422528 | tf_op jit(solution)/shard_map/slice | solution.py:45
  100.1 2.2 %fusion.17 = (bf16[4,1,4,28,2,896]{5,4,3,2,1,0:T(2,128)(2,1)S(1)}, bf16[4,1,4,28,2,896]{5,4,3,2,1,0:T(2,128)(2,1)S(1)}) fusion(bf16[4,2,4,28,2,896]{5,4,3,2,1,0:T(2,128)(2,1)S(1)} %reshape.88), kind=kLoop, calls=%fused_computation.32 | loop fusion | bytes 6422528 | tf_op jit(solution)/shard_map/slice | solution.py:45
  102.3 0.5 fusion.2
  102.8 0.5 fusion.3
  103.3 2.3 %maximum_bitcast_fusion = bf16[2,4,4,2,28,896]{5,4,3,2,1,0:T(8,128)(2,1)} fusion(bf16[1,4,4,28,2,896]{5,3,0,1,2,4:T(8,128)(2,1)S(1)} %fusion.3, bf16[1,4,4,28,2,896]{5,3,0,1,2,4:T(8,128)(2,1)S(1)} %fusion.2), kind=kLoop, calls=%fused_computation | loop fusion | flops 1605632 | bytes 6422528 | tf_op jit(solution)/shard_map/convert_element_type | solution.py:48
  105.6 6.0 %reshape.89 = bf16[1792,896]{1,0:T(8,128)(2,1)} reshape(bf16[2,4,4,2,28,896]{5,4,3,2,1,0:T(8,128)(2,1)} %maximum_bitcast_fusion) | data formatting | bytes 6422528 | tf_op jit(solution)/shard_map/reshape | solution.py:49
  111.6 0.0 reduce-scatter.2.cloned.1.call-update
  111.6 47.7 %reduce-scatter.2.cloned.1.call-done = bf16[224,896]{1,0:T(8,128)(2,1)} async-done(((bf16[1792,896]{1,0:T(8,128)(2,1)}), bf16[224,896]{1,0:T(8,128)(2,1)}) %reduce-scatter.2.cloned.1.call-update) | async-done | bytes 401424 | tf_op jit(solution)/shard_map/reduce_scatter | solution.py:50
  159.3 11.7 %all_to_all.5 = bf16[4,56,896]{2,1,0:T(8,128)(2,1)S(1)} all-to-all(bf16[4,56,896]{2,1,0:T(8,128)(2,1)} %bitcast.20), channel_id=1, replica_groups=mesh['task'=4,'z'=8,'yh'=2,'x'=4,'core'=2] {'x'}, dimensions={0} | all-to-all | bytes 802816 | tf_op jit(solution)/shard_map/all_to_all | solution.py:52
  171.0 0.1 convert_reduce_fusion
  171.1 0.7 broadcast_in_dim.5
  171.8 0.7 broadcast_in_dim.4
  (3 shorter events, 0.0 us)
Async XLA Ops:
  7.2 1.5 copy-start
  7.2 64.9 %all-gather.2.cloned.1.call-start = ((), (), s32[]{:S(2)}) async-start(), calls=%async_computation.2 | async-start | bytes 7798784 | tf_op jit(solution)/shard_map/all_gather | solution.py:36
  13.2 146.0 %reduce-scatter.2.cloned.1.call-start = ((), (), s32[]{:S(2)}) async-start(), calls=%async_computation.3 | async-start | bytes 3612672 | tf_op jit(solution)/shard_map/reduce_scatter | solution.py:50
Sparse Core Ops, SparseCore 0:
  13.4 58.7 all-gather.1
  111.7 47.4 reduce-scatter.1
where the time goes:
time: 180 us; the launch traced here: 179 us
  waiting for transfers between devices  106 us (59%)
  local copies, waits for them, and re-layouts  27.3 us (15%)
  between operations  14.2 us (8%)
  blocking collectives  11.7 us (6%)
  matrix products  10.8 us (6%)
  other arithmetic  8.75 us (5%)
    all_gather x1, waiting for transfers between devices, per_device(): seen = lax.all_gather(both, ('z', 'core'), axis=0, tiled=True)  58.8 us
    reduce_scatter x1, waiting for transfers between devices, per_device(): ring = lax.psum_scatter(parts, YRING, scatter_dimension=0, tiled=True)  47.7 us
    reshape x2, local copies, waits for them, and re-layouts, tile(): full = full.reshape(n_x, n_core, n_task, part, n_yh, band)  13 us
    all_to_all x1, blocking collectives, per_device(): ring = lax.all_to_all(ring, 'x', split_axis=0, concat_axis=0, tiled=True)  11.7 us
    dot_general x2, matrix products, tile(): lax.dot_general(left, right, (((0,), (0,)), ((), ())), preferred_element_...  10.8 us
    slice x2, local copies, waits for them, and re-layouts, tile(): return jnp.where(core == 0, full[:, 0], full[:, 1])  6.31 us
    reshape x1, local copies, waits for them, and re-layouts, per_device(): parts = parts.reshape(n_yh * n_task * n_x * 2 * part, band)  6 us
  transfers between devices with their start and end apart: 2, of which 2 were waited for; matrix products, arithmetic and copies ran while one was open for 0% of the time, Pallas kernels for 0%

commit v1 on v0

--- a/solution.py
+++ b/solution.py
@@ -33,7 +33,10 @@
     mixed = first + attn_out[0].astype(jnp.float32)
     x_mlp = (normed(mixed, gain_mlp) * live).astype(jnp.bfloat16)
     both = jnp.concatenate([x_attn, x_mlp], axis=1)
-    seen = lax.all_gather(both, ("z", "core"), axis=0, tiled=True)
+    seen = jnp.concatenate(
+        lax.all_to_all(jnp.stack([both] * lax.axis_size(("z", "core"))), ("z", "core"), 0, 0),
+        axis=0,
+    )
 
     def tile(at):
         left = lax.dynamic_slice_in_dim(seen, at * width + z // 2 * band, band, 1)

time: 180 us -> 296 us (1.64)
  waiting for transfers between devices: 106 us -> 210 us
  starting transfers between devices: 0.08 us -> 10.5 us
    all_to_all x0 -> x1, waiting for transfers between devices: none -> 162 us  [per_device(): lax.all_to_all(jnp.stack([both] * lax.axis_size(('z', 'core'))), ('z', 'c...]
    all_gather x1 -> x0, waiting for transfers between devices: 58.8 us -> none  [per_device(): seen = lax.all_gather(both, ('z', 'core'), axis=0, tiled=True)]
    all_to_all x0 -> x1, starting transfers between devices: none -> 10.5 us  [per_device(): lax.all_to_all(jnp.stack([both] * lax.axis_size(('z', 'core'))), ('z', 'c...]
    another operation x0 -> x1, local copies, waits for them, and re-layouts: none -> 3.9 us  [per_device(): jnp.stack([both] * lax.axis_size(('z', 'core')))]
where the time goes in v1:
time: 296 us; the launch traced here: 295 us
  waiting for transfers between devices  210 us (71%)
  local copies, waits for them, and re-layouts  29.9 us (10%)
  between operations  14.2 us (5%)
  blocking collectives  11.5 us (4%)
  matrix products  10.8 us (4%)
  starting transfers between devices  10.5 us (4%)
  other arithmetic  7.99 us (3%)
    all_to_all x1, waiting for transfers between devices, per_device(): lax.all_to_all(jnp.stack([both] * lax.axis_size(('z', 'core'))), ('z', 'c...  162 us
    reduce_scatter x1, waiting for transfers between devices, per_device(): ring = lax.psum_scatter(parts, YRING, scatter_dimension=0, tiled=True)  48.5 us
    reshape x2, local copies, waits for them, and re-layouts, tile(): full = full.reshape(n_x, n_core, n_task, part, n_yh, band)  11.8 us
    all_to_all x1, blocking collectives, per_device(): ring = lax.all_to_all(ring, 'x', split_axis=0, concat_axis=0, tiled=True)  11.5 us
    dot_general x2, matrix products, tile(): lax.dot_general(left, right, (((0,), (0,)), ((), ())), preferred_element_...  10.8 us
    all_to_all x1, starting transfers between devices, per_device(): lax.all_to_all(jnp.stack([both] * lax.axis_size(('z', 'core'))), ('z', 'c...  10.5 us
    slice x2, local copies, waits for them, and re-layouts, tile(): return jnp.where(core == 0, full[:, 0], full[:, 1])  6.18 us
    reshape x1, local copies, waits for them, and re-layouts, per_device(): parts = parts.reshape(n_yh * n_task * n_x * 2 * part, band)  6.02 us
  transfers between devices with their start and end apart: 2, of which 2 were waited for; matrix products, arithmetic and copies ran while one was open for 0% of the time, Pallas kernels for 0%

profile of v1, /device:TPU:24, one launch (start us, length us, event | category | flops | bytes accessed | tf_op | source)
XLA Modules:
  0.0 295.1 jit_solution(10196504562488684678)
XLA Ops:
  7.2 0.0 copy-start
  7.2 0.7 convert_element_type.40
  7.9 0.7 convert_element_type.45
  8.6 0.0 copy-done
  8.6 0.6 constant_dynamic-slice_fusion
  9.2 0.6 compare_convert_fusion
  9.8 1.3 fusion.10
  11.1 1.3 fusion.13
  12.4 3.9 %stack.5 = bf16[16,32,7168]{2,1,0:T(8,128)(2,1)} broadcast(bf16[32,7168]{1,0:T(8,128)(2,1)S(1)} %pad_maximum_fusion), dimensions={1,2} | broadcast | bytes 7798784 | tf_op jit(solution)/shard_map/stack | solution.py:37
  16.3 10.5 %all-to-all-start = ((bf16[16,32,7168]{2,1,0:T(8,128)(2,1)}), bf16[16,32,7168]{2,1,0:T(8,128)(2,1)}, u32[]{:S(2)}, u32[]{:S(2)}) async-start(bf16[16,32,7168]{2,1,0:T(8,128)(2,1)} %stack.5), calls=%async_computation | async-start | bytes 14680064 | tf_op jit(solution)/shard_map/all_to_all | solution.py:37
  26.8 0.0 reduce-scatter.2.cloned.1.call-start
  26.9 161.7 %all-to-all-done = bf16[16,32,7168]{2,1,0:T(8,128)(2,1)} async-done(((bf16[16,32,7168]{2,1,0:T(8,128)(2,1)}), bf16[16,32,7168]{2,1,0:T(8,128)(2,1)}, u32[]{:S(2)}, u32[]{:S(2)}) %all-to-all-start) | async-done | bytes 7340064 | tf_op jit(solution)/shard_map/all_to_all | solution.py:37
  188.5 5.4 %fusion.6 = bf16[896,1792]{1,0:T(8,128)(2,1)} fusion(bf16[512,7168]{1,0:T(8,128)(2,1)} %bitcast.4, s32[]{:T(128)S(6)} %select_n.71, s32[]{:T(128)S(6)} %select_n.69), kind=kOutput, calls=%fused_computation.9 | convolution fusion | flops 1644167168 | bytes 5963784 | tf_op jit(solution)/shard_map/dot_general | solution.py:44
  193.9 5.9 %reshape.93 = bf16[4,2,4,28,2,896]{5,4,3,2,1,0:T(2,128)(2,1)S(1)} reshape(bf16[896,1792]{1,0:T(8,128)(2,1)} %fusion.6) | data formatting | bytes 6422528 | tf_op jit(solution)/shard_map/reshape | solution.py:47
  199.8 4.0 %fusion.16 = (bf16[4,1,4,28,2,896]{5,4,3,2,1,0:T(2,128)(2,1)}, bf16[4,1,4,28,2,896]{5,4,3,2,1,0:T(2,128)(2,1)}) fusion(bf16[4,2,4,28,2,896]{5,4,3,2,1,0:T(2,128)(2,1)S(1)} %reshape.93), kind=kLoop, calls=%fused_computation.31 | loop fusion | bytes 6422528 | tf_op jit(solution)/shard_map/slice | solution.py:48
  203.8 5.4 %fusion.4 = bf16[896,1792]{1,0:T(8,128)(2,1)} fusion(bf16[512,7168]{1,0:T(8,128)(2,1)} %bitcast.4, s32[]{:T(128)S(6)} %select_n.75, s32[]{:T(128)S(6)} %select_n.74), kind=kOutput, calls=%fused_computation.7 | convolution fusion | flops 1644167168 | bytes 5963784 | tf_op jit(solution)/shard_map/dot_general | solution.py:44
  209.2 5.9 %reshape.94 = bf16[4,2,4,28,2,896]{5,4,3,2,1,0:T(2,128)(2,1)S(1)} reshape(bf16[896,1792]{1,0:T(8,128)(2,1)} %fusion.4) | data formatting | bytes 6422528 | tf_op jit(solution)/shard_map/reshape | solution.py:47
  215.1 0.0 copy-start.1
  215.1 0.0 copy-start.2
  215.1 2.2 fusion.17
  217.4 0.0 copy-done.1
  217.4 0.0 copy-done.2
  217.4 0.5 fusion.2
  217.9 0.5 fusion.3
  218.4 2.3 maximum_bitcast_fusion
  220.7 6.0 %reshape.95 = bf16[1792,896]{1,0:T(8,128)(2,1)} reshape(bf16[2,4,4,2,28,896]{5,4,3,2,1,0:T(8,128)(2,1)} %maximum_bitcast_fusion) | data formatting | bytes 6422528 | tf_op jit(solution)/shard_map/reshape | solution.py:52
  226.7 0.0 reduce-scatter.2.cloned.1.call-update
  226.7 48.5 %reduce-scatter.2.cloned.1.call-done = bf16[224,896]{1,0:T(8,128)(2,1)} async-done(((bf16[1792,896]{1,0:T(8,128)(2,1)}), bf16[224,896]{1,0:T(8,128)(2,1)}) %reduce-scatter.2.cloned.1.call-update) | async-done | bytes 401424 | tf_op jit(solution)/shard_map/reduce_scatter | solution.py:53
  275.2 11.5 %all_to_all.10 = bf16[4,56,896]{2,1,0:T(8,128)(2,1)S(1)} all-to-all(bf16[4,56,896]{2,1,0:T(8,128)(2,1)} %bitcast.21), channel_id=1, replica_groups=mesh['task'=4,'z'=8,'yh'=2,'x'=4,'core'=2] {'x'}, dimensions={0} | all-to-all | bytes 802816 | tf_op jit(solution)/shard_map/all_to_all | solution.py:55
  286.7 0.1 convert_reduce_fusion
  286.8 0.7 broadcast_in_dim.4
  287.5 0.7 broadcast_in_dim.5
  (4 shorter events, 0.1 us)
Async XLA Ops:
  7.2 1.4 copy-start
  16.3 172.2 %all-to-all-start = ((bf16[16,32,7168]{2,1,0:T(8,128)(2,1)}), bf16[16,32,7168]{2,1,0:T(8,128)(2,1)}, u32[]{:S(2)}, u32[]{:S(2)}) async-start(bf16[16,32,7168]{2,1,0:T(8,128)(2,1)} %stack.5), calls=%async_computation | async-start | bytes 14680064 | tf_op jit(solution)/shard_map/all_to_all | solution.py:37
  26.8 248.4 %reduce-scatter.2.cloned.1.call-start = ((), (), s32[]{:S(2)}) async-start(), calls=%async_computation.3 | async-start | bytes 3612672 | tf_op jit(solution)/shard_map/reduce_scatter | solution.py:53
  215.1 2.2 copy-start.1
  215.1 2.2 copy-start.2
Sparse Core Ops, SparseCore 0:
  226.9 48.3 reduce-scatter.1
